TPU v7x, 32 devices: a whole 2x2x4 slice. The times are simulated.
32 devices in a mesh: rows: 8 (over z, y), cols: 4 (over x, core).
Axes of the slice: x: 2, y: 2, z: 4, core: 2. Of those that a mesh axis runs over, the one named last changes fastest.
Arguments:
- latent: bfloat16 [4, 8, 1024], P(None, 'rows', 'cols'), may hold values from -18 to 18
- deep: bfloat16 [320, 8, 1024], P(None, 'rows', 'cols'), may hold values from -6 to 6
- timestep: int32 [1], replicated, may hold values from 0 to 999
- in_weight: bfloat16 [36, 320], replicated, may hold values from -1 to 1
- front_weight: bfloat16 [5760, 320], P('rows'), may hold values from -0.078125 to 0.078125
- middle_weight: bfloat16 [2880, 320], P('cols'), may hold values from -0.109375 to 0.109375
- skip_weight: bfloat16 [640, 320], P('cols'), may hold values from -0.25 to 0.25
- out_weight: bfloat16 [2880, 4], replicated, may hold values from -0.109375 to 0.109375
- time_weight: bfloat16 [320, 1280], replicated, may hold values from -0.3125 to 0.3125
- time_second: bfloat16 [1280, 1280], P('cols'), may hold values from -0.15625 to 0.15625
- time_proj: bfloat16 [1280, 320], replicated, may hold values from -0.15625 to 0.15625
- input_gain: float32 [640], replicated, may hold values from 0.1 to 1.9
- middle_gain: float32 [320], replicated, may hold values from 0.1 to 1.9
- output_gain: float32 [320], replicated, may hold values from 0.1 to 1.9
Outputs:
- noise: float32 [4, 8, 1024], P(None, 'rows', 'cols')
All inputs are finite; a program needn't handle non-finite values.
Results may differ from a plain program's by a relative error of at most 0.0047.
Values may be sent and summed in bfloat16 or wider, within the bound.
A program may use at most 64 MiB of HBM per device.

v0:
```python
import math

import jax
import jax.numpy as jnp
from jax import lax
from jax.sharding import PartitionSpec as P

GROUPS = 32


epsilon = 1e-05


def padded_2(cells, sides, width):
    for axis, dim in sides:
        count = lax.axis_size(axis)
        ends = count - 1
        head = lax.slice_in_dim(cells, 0, width, axis=dim)
        tail = lax.slice_in_dim(cells, cells.shape[dim] - width, cells.shape[dim], axis=dim)
        cells = jnp.concatenate(
            [
                lax.ppermute(tail, axis, [(i, (i + 1) % count) for i in range(ends)]),
                cells,
                lax.ppermute(head, axis, [((i + 1) % count, i) for i in range(ends)]),
            ],
            axis=dim,
        )
    return cells


def unfold(padded, row_count, col_count):
    shifted = [
        padded[:, row_step : row_step + row_count, col_step : col_step + col_count]
        for row_step in range(3)
        for col_step in range(3)
    ]
    return jnp.stack(shifted, 0).reshape(9 * padded.shape[0], row_count * col_count)


def project(weight, columns):
    return lax.dot_general(
        weight, columns, (((0,), (0,)), ((), ())), preferred_element_type=jnp.float32
    )


def norm_silu(values, gain, members):
    grouped = values.reshape(GROUPS, -1)
    totals, squares = lax.psum(
        (jnp.sum(grouped, axis=1), jnp.sum(grouped * grouped, axis=1)), ("rows", "cols")
    )
    center = totals / members
    offsets = grouped - center[:, None]
    spread = squares / members - center * center
    scaled = (offsets * lax.rsqrt(spread + epsilon)[:, None]).reshape(values.shape) * gain[:, None]
    return jax.nn.silu(scaled).astype(jnp.bfloat16)


def time_shift_of(timestep, time_weight, time_second, time_proj):
    half_width = time_weight.shape[0] // 2
    ratios = jnp.exp(-math.log(10000.0) * jnp.arange(half_width, dtype=jnp.float32) / half_width)
    angles = timestep[0].astype(jnp.float32) * ratios
    features = jnp.concatenate([jnp.cos(angles), jnp.sin(angles)])
    hidden = jax.nn.silu(
        jnp.dot(features, time_weight.astype(jnp.float32), precision=lax.Precision.HIGHEST)
    )
    embedded = jnp.dot(hidden, time_second.astype(jnp.float32), precision=lax.Precision.HIGHEST)
    return jnp.dot(
        jax.nn.silu(embedded), time_proj.astype(jnp.float32), precision=lax.Precision.HIGHEST
    )


def shards(
    latent,
    deep,
    timestep,
    in_weight,
    front_weight,
    middle_weight,
    skip_weight,
    out_weight,
    time_weight,
    time_second,
    time_proj,
    input_gain,
    middle_gain,
    output_gain,
):
    rows_here = latent.shape[1]
    cols_here = latent.shape[2]
    pixels = rows_here * cols_here
    image_cells = pixels * lax.axis_size("rows") * lax.axis_size("cols")
    channels = deep.shape[0]
    full_middle, full_skip, full_second = (
        lax.all_gather(middle_weight, "cols", axis=0, tiled=True),
        lax.all_gather(skip_weight, "cols", axis=0, tiled=True),
        lax.all_gather(time_second, "cols", axis=0, tiled=True),
    )
    time_shift = time_shift_of(timestep, time_weight, full_second, time_proj)
    padded_latent = padded_2(latent, (("rows", 1), ("cols", 2)), 1)
    skip_feat = project(in_weight, unfold(padded_latent, rows_here, cols_here)).astype(jnp.bfloat16)
    joined = jnp.concatenate([deep.reshape(channels, pixels), skip_feat], axis=0)
    members_wide = float(joined.shape[0] // GROUPS * image_cells)
    act_one = norm_silu(joined.astype(jnp.float32), input_gain, members_wide)
    padded_one = padded_2(act_one.reshape(-1, rows_here, cols_here), (("rows", 1), ("cols", 2)), 1)
    columns_one = unfold(padded_one, rows_here, cols_here)
    out_channels = front_weight.shape[1]
    hidden_one = project(lax.all_gather(front_weight, "rows", axis=0, tiled=True), columns_one)
    hidden_one = hidden_one + time_shift[:, None]
    members_narrow = float(out_channels // GROUPS * image_cells)
    act_two = norm_silu(hidden_one, middle_gain, members_narrow)
    padded_two = padded_2(act_two.reshape(-1, rows_here, cols_here), (("rows", 1), ("cols", 2)), 1)
    block_out = project(full_middle, unfold(padded_two, rows_here, cols_here)) + project(
        full_skip, joined
    )
    act_three = norm_silu(block_out, output_gain, members_narrow)
    padded_three = padded_2(
        act_three.reshape(-1, rows_here, cols_here), (("rows", 1), ("cols", 2)), 1
    )
    noise = project(out_weight, unfold(padded_three, rows_here, cols_here))
    return noise.reshape(out_weight.shape[1], rows_here, cols_here)


def solution(mesh):
    return jax.shard_map(
        shards,
        mesh=mesh,
        in_specs=(
            P(None, "rows", "cols"),
            P(None, "rows", "cols"),
            P(),
            P(),
            P("rows", None),
            P("cols", None),
            P("cols", None),
            P(),
            P(),
            P("cols", None),
            P(),
            P(),
            P(),
            P(),
        ),
        out_specs=P(None, "rows", "cols"),
        check_vma=False,
    )
```

profile of v0, /device:TPU:1, one launch (start us, length us, event | category | flops | bytes accessed | tf_op | source)
XLA Modules:
  0.0 288.9 jit_solution(18141024162839001705)
XLA Ops:
  8.1 4.0 %collective-permute-start = (bf16[4,1,256]{2,0,1:T(4,128)(2,1)}, bf16[4,1,256]{2,0,1:T(4,128)(2,1)S(1)}, u32[]{:S(2)}, u32[]{:S(2)}) collective-permute-start(bf16[4,1,256]{2,0,1:T(4,128)(2,1)} %param.14), channel_id=1, source_target_pairs={{0,4},{4,8},{8,12},{12,16},{16,20},{20,24},{24,28},{1,5},{5,9},{9,... | collective-permute-start | bytes 6152 | tf_op jit(solution)/shard_map/ppermute | solution.py:22
  12.0 1.3 collective-permute-start.1
  14.1 2.5 collective-permute-done.1
  16.7 5.1 %collective-permute-start.2 = (bf16[4,3,1]{2,0,1:T(4,128)(2,1)S(1)}, bf16[4,3,1]{2,0,1:T(4,128)(2,1)S(1)}, u32[]{:S(2)}, u32[]{:S(2)}) collective-permute-start(bf16[4,3,1]{2,0,1:T(4,128)(2,1)S(1)} %get-tuple-element.24), channel_id=1, source_target_pairs={{0,1},{1,2},{2,3},{4,5},{5,6},{6,7},{8,9},{9,10},{10,11},{12,13},{... | collective-permute-start | bytes 80 | tf_op jit(solution)/shard_map/ppermute | solution.py:22
  21.8 1.9 collective-permute-start.3
  23.8 3.5 %collective-permute-done.3 = bf16[4,3,1]{2,0,1:T(4,128)(2,1)S(1)} collective-permute-done((bf16[4,3,1]{2,0,1:T(4,128)(2,1)S(1)}, bf16[4,3,1]{2,0,1:T(4,128)(2,1)S(1)}, u32[]{:S(2)}, u32[]{:S(2)}) %collective-permute-start.3) | collective-permute-done | bytes 56 | tf_op jit(solution)/shard_map/ppermute | solution.py:24
  28.7 41.0 %all-reduce.2 = (f32[32]{0:T(128)S(1)}, f32[32]{0:T(128)S(1)}) all-reduce(f32[32]{0:T(128)S(1)} %reduce_sum.77, f32[32]{0:T(128)S(1)} %reduce_sum.74), channel_id=1, replica_groups=mesh['rows'=8,'cols'=4] {'rows','cols'}, use_global_device_ids=true, to_apply=%region_5.6 | all-reduce | flops 64 | bytes 512 | tf_op jit(solution)/shard_map/psum | solution.py:48
  70.4 1.7 collective-permute-start.4
  72.1 1.3 collective-permute-start.5
  74.0 2.1 collective-permute-done.4
  76.0 9.4 %collective-permute-done.5 = bf16[640,1,256]{2,0,1:T(8,128)(2,1)S(1)} collective-permute-done((bf16[640,1,256]{2,0,1:T(8,128)(2,1)S(1)}, bf16[640,1,256]{2,0,1:T(8,128)(2,1)S(1)}, u32[]{:S(2)}, u32[]{:S(2)}) %collective-permute-start.5) | collective-permute-done | bytes 327712 | tf_op jit(solution)/shard_map/ppermute | solution.py:24
  85.8 9.4 %collective-permute-start.6 = (bf16[640,3,1]{2,0,1:T(8,128)(2,1)S(1)}, bf16[640,3,1]{2,0,1:T(8,128)(2,1)S(1)}, u32[]{:S(2)}, u32[]{:S(2)}) collective-permute-start(bf16[640,3,1]{2,0,1:T(8,128)(2,1)S(1)} %get-tuple-element.18), channel_id=1, source_target_pairs={{0,1},{1,2},{2,3},{4,5},{5,6},{6,7},{8,9},{9,10},{10,11},{12,13},{... | collective-permute-start | bytes 11528 | tf_op jit(solution)/shard_map/ppermute | solution.py:22
  95.3 1.9 collective-permute-start.7
  97.2 3.8 %collective-permute-done.6 = bf16[640,3,1]{2,0,1:T(8,128)(2,1)S(1)} collective-permute-done((bf16[640,3,1]{2,0,1:T(8,128)(2,1)S(1)}, bf16[640,3,1]{2,0,1:T(8,128)(2,1)S(1)}, u32[]{:S(2)}, u32[]{:S(2)}) %collective-permute-start.6) | collective-permute-done | bytes 3872 | tf_op jit(solution)/shard_map/ppermute | solution.py:22
  102.7 2.7 collective-permute-done.7
  105.4 1.0 fusion.8
  106.4 0.9 fusion.7
  107.3 1.1 fusion.1
  108.4 0.9 fusion.6
  109.3 0.9 fusion.5
  110.9 0.9 fusion.3
  111.9 3.4 %convolution_reduce_fusion = f32[1280]{0:T(1024)S(1)} fusion(f32[1280,1]{0,1:T(1,128)S(1)} %reshape.325, bf16[1280,1280]{1,0:T(8,128)(2,1)} %all-gather.6.cloned.1.call-done), kind=kOutput, calls=%fused_computation.3 | convolution fusion | flops 19660800 | bytes 3287040 | tf_op jit(solution)/shard_map/dot_general | solution.py:66
  116.1 6.8 %all-gather.8.cloned.1.call-done = bf16[8,720,320]{1,2,0:T(8,128)(2,1)} async-done(((bf16[1,720,320]{1,2,0:T(8,128)(2,1)}), bf16[8,720,320]{1,2,0:T(8,128)(2,1)}) %all-gather.8.cloned.1.call-update) | async-done | bytes 3686416 | tf_op jit(solution)/shard_map/all_gather | solution.py:107
  122.9 6.2 %copy.19 = bf16[8,720,320]{1,0,2:T(8,128)(2,1)} copy(bf16[8,720,320]{1,2,0:T(8,128)(2,1)} %all-gather.8.cloned.1.call-done) | data formatting | bytes 7372800 | tf_op jit(solution)/shard_map/all_gather | solution.py:107
  129.1 7.9 %reshape.320 = bf16[5760,320]{0,1:T(8,128)(2,1)} reshape(bf16[8,720,320]{1,0,2:T(8,128)(2,1)} %copy.19) | data formatting | bytes 7372800
  137.1 4.3 %fusion.41 = (f32[320]{0:T(512)S(1)}, f32[320]{0:T(512)S(1)}, f32[256,320]{0,1:T(8,128)S(1)}) fusion(f32[320]{0:T(512)S(1)} %convolution_reduce_fusion.2, bf16[5760,320]{0,1:T(8,128)(2,1)} %reshape.320, bf16[5760,256]{1,0:T(8,128)(2,1)} %bitcast.22), kind=kOutput, calls=%fused_computation.128 | convolution fusion | flops 944045440 | bytes 6967040 | tf_op jit(solution)/shard_map/dot_general | solution.py:41
  141.8 39.3 %all-reduce.1 = (f32[32]{0:T(128)S(1)}, f32[32]{0:T(128)S(1)}) all-reduce(f32[32]{0:T(128)S(1)} %reduce_sum.89, f32[32]{0:T(128)S(1)} %reduce_sum.83), channel_id=1, replica_groups=mesh['rows'=8,'cols'=4] {'rows','cols'}, use_global_device_ids=true, to_apply=%region_11.12 | all-reduce | flops 64 | bytes 512 | tf_op jit(solution)/shard_map/psum | solution.py:48
  181.8 2.6 collective-permute-start.8
  184.3 1.3 collective-permute-start.9
  185.7 9.4 %all_gather.15 = bf16[640,320]{1,0:T(8,128)(2,1)S(1)} all-gather(bf16[160,320]{1,0:T(8,128)(2,1)S(1)} %copy-done.7), channel_id=1, replica_groups=mesh['rows'=8,'cols'=4] {'cols'}, dimensions={0}, use_global_device_ids=true | all-gather | bytes 512000 | tf_op jit(solution)/shard_map/all_gather | solution.py:95
  196.0 2.8 collective-permute-start.10
  198.8 1.1 fusion.34
  199.9 3.1 %copy.20 = bf16[4,720,320]{1,0,2:T(4,128)(2,1)S(1)} copy(bf16[4,720,320]{1,2,0:T(8,128)(2,1)} %all-gather.10.cloned.1.call-done) | data formatting | bytes 3686400 | tf_op jit(solution)/shard_map/all_gather | solution.py:94
  202.9 2.6 reshape.322
  205.6 2.3 collective-permute-start.11
  207.9 1.0 fusion.33
  208.9 4.5 %collective-permute-done.11 = bf16[320,3,1]{2,0,1:T(8,128)(2,1)S(1)} collective-permute-done((bf16[320,3,1]{2,0,1:T(8,128)(2,1)}, bf16[320,3,1]{2,0,1:T(8,128)(2,1)S(1)}, u32[]{:S(2)}, u32[]{:S(2)}) %collective-permute-start.11) | collective-permute-done | bytes 1952 | tf_op jit(solution)/shard_map/ppermute | solution.py:24
  213.5 1.0 fusion.31
  215.0 1.1 fusion.29
  217.6 38.1 %all-reduce = (f32[32]{0:T(128)S(1)}, f32[32]{0:T(128)S(1)}) all-reduce(f32[32]{0:T(128)S(1)} %reduce_sum.113, f32[32]{0:T(128)S(1)} %reduce_sum.110), channel_id=1, replica_groups=mesh['rows'=8,'cols'=4] {'rows','cols'}, use_global_device_ids=true, to_apply=%region_17.18 | all-reduce | flops 64 | bytes 512 | tf_op jit(solution)/shard_map/psum | solution.py:48
  256.3 4.2 %collective-permute-start.12 = (bf16[320,1,256]{2,0,1:T(8,128)(2,1)S(1)}, bf16[320,1,256]{2,0,1:T(8,128)(2,1)S(1)}, u32[]{:S(2)}, u32[]{:S(2)}) collective-permute-start(bf16[320,1,256]{2,0,1:T(8,128)(2,1)S(1)} %fusion.61), channel_id=1, source_target_pairs={{0,4},{4,8},{8,12},{12,16},{16,20},{20,24},{24,28},{1,5},{5,9},{9,... | collective-permute-start | bytes 491528 | tf_op jit(solution)/shard_map/ppermute | solution.py:22
  260.5 1.3 collective-permute-start.13
  261.8 0.9 collective-permute-done.12
  262.7 3.8 %collective-permute-done.13 = bf16[320,1,256]{2,0,1:T(8,128)(2,1)S(1)} collective-permute-done((bf16[320,1,256]{2,0,1:T(8,128)(2,1)S(1)}, bf16[320,1,256]{2,0,1:T(8,128)(2,1)S(1)}, u32[]{:S(2)}, u32[]{:S(2)}) %collective-permute-start.13) | collective-permute-done | bytes 163872 | tf_op jit(solution)/shard_map/ppermute | solution.py:24
  266.8 5.9 %collective-permute-start.14 = (bf16[320,3,1]{2,0,1:T(8,128)(2,1)S(1)}, bf16[320,3,1]{2,0,1:T(8,128)(2,1)S(1)}, u32[]{:S(2)}, u32[]{:S(2)}) collective-permute-start(bf16[320,3,1]{2,0,1:T(8,128)(2,1)S(1)} %get-tuple-element.20), channel_id=1, source_target_pairs={{0,1},{1,2},{2,3},{4,5},{5,6},{6,7},{8,9},{9,10},{10,11},{12,13},{... | collective-permute-start | bytes 5768 | tf_op jit(solution)/shard_map/ppermute | solution.py:22
  272.7 1.9 collective-permute-start.15
  274.6 1.2 collective-permute-done.14
  275.9 4.3 %collective-permute-done.15 = bf16[320,3,1]{2,0,1:T(8,128)(2,1)S(1)} collective-permute-done((bf16[320,3,1]{2,0,1:T(8,128)(2,1)S(1)}, bf16[320,3,1]{2,0,1:T(8,128)(2,1)S(1)}, u32[]{:S(2)}, u32[]{:S(2)}) %collective-permute-start.15) | collective-permute-done | bytes 1952 | tf_op jit(solution)/shard_map/ppermute | solution.py:24
  (123 shorter events, 14.9 us)
Async XLA Ops:
  6.5 67.0 %copy-start = (bf16[320,1280]{1,0:T(8,128)(2,1)S(1)}, bf16[320,1280]{1,0:T(8,128)(2,1)}, u32[]{:S(2)}) copy-start(bf16[320,1280]{1,0:T(8,128)(2,1)} %param.22) | copy-start | bytes 2457604
  6.5 7.5 %copy-start.13 = (bf16[4,1,256]{2,0,1:T(4,128)(2,1)S(1)}, bf16[4,1,256]{2,0,1:T(4,128)(2,1)}, u32[]{:S(2)}) copy-start(bf16[4,1,256]{2,0,1:T(4,128)(2,1)} %param.14) | copy-start | bytes 6148
  6.5 21.2 %copy-start.8 = (bf16[36,320]{1,0:T(8,128)(2,1)S(1)}, bf16[36,320]{1,0:T(8,128)(2,1)}, u32[]{:S(2)}) copy-start(bf16[36,320]{1,0:T(8,128)(2,1)} %param.17) | copy-start | bytes 69124
  6.5 21.5 %copy-start.1 = (bf16[320,1,256]{2,0,1:T(8,128)(2,1)S(1)}, bf16[320,1,256]{2,0,1:T(8,128)(2,1)}, u32[]{:S(2)}) copy-start(bf16[320,1,256]{2,0,1:T(8,128)(2,1)} %param.15) | copy-start | bytes 491524
  6.5 63.5 %copy-start.10 = (f32[640]{0:T(1024)S(1)}, f32[640]{0:T(1024)}, u32[]{:S(2)}) copy-start(f32[640]{0:T(1024)} %param.25) | copy-start | bytes 7684
  6.5 105.3 %all-gather.6.cloned.1.call-start = ((), (), s32[]{:S(2)}) async-start(), calls=%async_computation | async-start | bytes 4096000 | tf_op jit(solution)/shard_map/all_gather | solution.py:96
  7.3 115.7 %all-gather.8.cloned.1.call-start = ((), (), s32[]{:S(2)}) async-start(), calls=%async_computation.1 | async-start | bytes 4423680 | tf_op jit(solution)/shard_map/all_gather | solution.py:107
  8.0 191.8 %all-gather.10.cloned.1.call-start = ((), (), s32[]{:S(2)}) async-start(), calls=%async_computation.2 | async-start | bytes 2457600 | tf_op jit(solution)/shard_map/all_gather | solution.py:94
  8.1 5.9 %collective-permute-start = (bf16[4,1,256]{2,0,1:T(4,128)(2,1)}, bf16[4,1,256]{2,0,1:T(4,128)(2,1)S(1)}, u32[]{:S(2)}, u32[]{:S(2)}) collective-permute-start(bf16[4,1,256]{2,0,1:T(4,128)(2,1)} %param.14), channel_id=1, source_target_pairs={{0,4},{4,8},{8,12},{12,16},{16,20},{20,24},{24,28},{1,5},{5,9},{9,... | collective-permute-start | bytes 6152 | tf_op jit(solution)/shard_map/ppermute | solution.py:22
  12.0 4.5 %collective-permute-start.1 = (bf16[4,1,256]{2,0,1:T(4,128)(2,1)}, bf16[4,1,256]{2,0,1:T(4,128)(2,1)S(1)}, u32[]{:S(2)}, u32[]{:S(2)}) collective-permute-start(bf16[4,1,256]{2,0,1:T(4,128)(2,1)} %param.14), channel_id=1, source_target_pairs={{4,0},{8,4},{12,8},{16,12},{20,16},{24,20},{28,24},{5,1},{9,5},{13... | collective-permute-start | bytes 6152 | tf_op jit(solution)/shard_map/ppermute | solution.py:24
  16.7 7.0 %collective-permute-start.2 = (bf16[4,3,1]{2,0,1:T(4,128)(2,1)S(1)}, bf16[4,3,1]{2,0,1:T(4,128)(2,1)S(1)}, u32[]{:S(2)}, u32[]{:S(2)}) collective-permute-start(bf16[4,3,1]{2,0,1:T(4,128)(2,1)S(1)} %get-tuple-element.24), channel_id=1, source_target_pairs={{0,1},{1,2},{2,3},{4,5},{5,6},{6,7},{8,9},{9,10},{10,11},{12,13},{... | collective-permute-start | bytes 80 | tf_op jit(solution)/shard_map/ppermute | solution.py:22
  21.8 5.5 %collective-permute-start.3 = (bf16[4,3,1]{2,0,1:T(4,128)(2,1)S(1)}, bf16[4,3,1]{2,0,1:T(4,128)(2,1)S(1)}, u32[]{:S(2)}, u32[]{:S(2)}) collective-permute-start(bf16[4,3,1]{2,0,1:T(4,128)(2,1)S(1)} %get-tuple-element.23), channel_id=1, source_target_pairs={{1,0},{2,1},{3,2},{5,4},{6,5},{7,6},{9,8},{10,9},{11,10},{13,12},{... | collective-permute-start | bytes 80 | tf_op jit(solution)/shard_map/ppermute | solution.py:24
  70.4 5.7 %collective-permute-start.4 = (bf16[640,1,256]{2,0,1:T(8,128)(2,1)S(1)}, bf16[640,1,256]{2,0,1:T(8,128)(2,1)S(1)}, u32[]{:S(2)}, u32[]{:S(2)}) collective-permute-start(bf16[640,1,256]{2,0,1:T(8,128)(2,1)S(1)} %multiply_convert_fusion.1), channel_id=1, source_target_pairs={{0,4},{4,8},{8,12},{12,16},{16,20},{20,24},{24,28},{1,5},{5,9},{9,... | collective-permute-start | bytes 983048 | tf_op jit(solution)/shard_map/ppermute | solution.py:22
  72.1 13.4 %collective-permute-start.5 = (bf16[640,1,256]{2,0,1:T(8,128)(2,1)S(1)}, bf16[640,1,256]{2,0,1:T(8,128)(2,1)S(1)}, u32[]{:S(2)}, u32[]{:S(2)}) collective-permute-start(bf16[640,1,256]{2,0,1:T(8,128)(2,1)S(1)} %multiply_convert_fusion.1), channel_id=1, source_target_pairs={{4,0},{8,4},{12,8},{16,12},{20,16},{24,20},{28,24},{5,1},{9,5},{13... | collective-permute-start | bytes 983048 | tf_op jit(solution)/shard_map/ppermute | solution.py:24
  85.8 15.2 %collective-permute-start.6 = (bf16[640,3,1]{2,0,1:T(8,128)(2,1)S(1)}, bf16[640,3,1]{2,0,1:T(8,128)(2,1)S(1)}, u32[]{:S(2)}, u32[]{:S(2)}) collective-permute-start(bf16[640,3,1]{2,0,1:T(8,128)(2,1)S(1)} %get-tuple-element.18), channel_id=1, source_target_pairs={{0,1},{1,2},{2,3},{4,5},{5,6},{6,7},{8,9},{9,10},{10,11},{12,13},{... | collective-permute-start | bytes 11528 | tf_op jit(solution)/shard_map/ppermute | solution.py:22
  95.3 10.1 %collective-permute-start.7 = (bf16[640,3,1]{2,0,1:T(8,128)(2,1)S(1)}, bf16[640,3,1]{2,0,1:T(8,128)(2,1)S(1)}, u32[]{:S(2)}, u32[]{:S(2)}) collective-permute-start(bf16[640,3,1]{2,0,1:T(8,128)(2,1)S(1)} %get-tuple-element.17), channel_id=1, source_target_pairs={{1,0},{2,1},{3,2},{5,4},{6,5},{7,6},{9,8},{10,9},{11,10},{13,12},{... | collective-permute-start | bytes 11528 | tf_op jit(solution)/shard_map/ppermute | solution.py:24
  111.9 3.4 %copy-start.5 = (bf16[1280,320]{0,1:T(8,128)(2,1)S(1)}, bf16[1280,320]{0,1:T(8,128)(2,1)}, u32[]{:S(2)}) copy-start(bf16[1280,320]{0,1:T(8,128)(2,1)} %param.24) | copy-start | bytes 2457604
  137.1 44.5 %copy-start.11 = (f32[320]{0:T(512)S(1)}, f32[320]{0:T(512)}, u32[]{:S(2)}) copy-start(f32[320]{0:T(512)} %param.26) | copy-start | bytes 3844
  137.1 48.6 %copy-start.7 = (bf16[160,320]{1,0:T(8,128)(2,1)S(1)}, bf16[160,320]{1,0:T(8,128)(2,1)}, u32[]{:S(2)}) copy-start(bf16[160,320]{1,0:T(8,128)(2,1)} %param.20) | copy-start | bytes 307204
  141.4 40.2 %copy-start.3 = (f32[256,320]{0,1:T(8,128)}, f32[256,320]{0,1:T(8,128)S(1)}, u32[]{:S(2)}) copy-start(f32[256,320]{0,1:T(8,128)S(1)} %get-tuple-element.31) | copy-start | bytes 983044
  181.8 13.2 %collective-permute-start.8 = (bf16[320,1,256]{2,0,1:T(8,128)(2,1)S(1)}, bf16[320,1,256]{2,0,1:T(8,128)(2,1)S(1)}, u32[]{:S(2)}, u32[]{:S(2)}) collective-permute-start(bf16[320,1,256]{2,0,1:T(8,128)(2,1)S(1)} %fusion.62), channel_id=1, source_target_pairs={{0,4},{4,8},{8,12},{12,16},{16,20},{20,24},{24,28},{1,5},{5,9},{9,... | collective-permute-start | bytes 491528 | tf_op jit(solution)/shard_map/ppermute | solution.py:22
  184.3 10.7 %collective-permute-start.9 = (bf16[320,1,256]{2,0,1:T(8,128)(2,1)S(1)}, bf16[320,1,256]{2,0,1:T(8,128)(2,1)S(1)}, u32[]{:S(2)}, u32[]{:S(2)}) collective-permute-start(bf16[320,1,256]{2,0,1:T(8,128)(2,1)S(1)} %fusion.62), channel_id=1, source_target_pairs={{4,0},{8,4},{12,8},{16,12},{20,16},{24,20},{28,24},{5,1},{9,5},{13... | collective-permute-start | bytes 491528 | tf_op jit(solution)/shard_map/ppermute | solution.py:24
  196.0 11.9 %collective-permute-start.10 = (bf16[320,3,1]{2,0,1:T(8,128)(2,1)}, bf16[320,3,1]{2,0,1:T(8,128)(2,1)}, u32[]{:S(2)}, u32[]{:S(2)}) collective-permute-start(bf16[320,3,1]{2,0,1:T(8,128)(2,1)} %get-tuple-element.22), channel_id=1, source_target_pairs={{0,1},{1,2},{2,3},{4,5},{5,6},{6,7},{8,9},{9,10},{10,11},{12,13},{... | collective-permute-start | bytes 5768 | tf_op jit(solution)/shard_map/ppermute | solution.py:22
  205.6 9.0 %copy-start.4 = (f32[256,320]{0,1:T(8,128)S(1)}, f32[256,320]{0,1:T(8,128)}, u32[]{:S(2)}) copy-start(f32[256,320]{0,1:T(8,128)} %copy-done.3) | copy-start | bytes 983044
  205.6 7.8 %collective-permute-start.11 = (bf16[320,3,1]{2,0,1:T(8,128)(2,1)}, bf16[320,3,1]{2,0,1:T(8,128)(2,1)S(1)}, u32[]{:S(2)}, u32[]{:S(2)}) collective-permute-start(bf16[320,3,1]{2,0,1:T(8,128)(2,1)} %get-tuple-element.21), channel_id=1, source_target_pairs={{1,0},{2,1},{3,2},{5,4},{6,5},{7,6},{9,8},{10,9},{11,10},{13,12},{... | collective-permute-start | bytes 5768 | tf_op jit(solution)/shard_map/ppermute | solution.py:24
  214.8 1.6 copy-start.2
  214.8 1.6 copy-start.6
  216.4 39.7 %copy-start.12 = (f32[320]{0:T(512)S(1)}, f32[320]{0:T(512)}, u32[]{:S(2)}) copy-start(f32[320]{0:T(512)} %param.27) | copy-start | bytes 3844
  256.3 6.4 %collective-permute-start.12 = (bf16[320,1,256]{2,0,1:T(8,128)(2,1)S(1)}, bf16[320,1,256]{2,0,1:T(8,128)(2,1)S(1)}, u32[]{:S(2)}, u32[]{:S(2)}) collective-permute-start(bf16[320,1,256]{2,0,1:T(8,128)(2,1)S(1)} %fusion.61), channel_id=1, source_target_pairs={{0,4},{4,8},{8,12},{12,16},{16,20},{20,24},{24,28},{1,5},{5,9},{9,... | collective-permute-start | bytes 491528 | tf_op jit(solution)/shard_map/ppermute | solution.py:22
  260.5 6.1 %collective-permute-start.13 = (bf16[320,1,256]{2,0,1:T(8,128)(2,1)S(1)}, bf16[320,1,256]{2,0,1:T(8,128)(2,1)S(1)}, u32[]{:S(2)}, u32[]{:S(2)}) collective-permute-start(bf16[320,1,256]{2,0,1:T(8,128)(2,1)S(1)} %fusion.61), channel_id=1, source_target_pairs={{4,0},{8,4},{12,8},{16,12},{20,16},{24,20},{28,24},{5,1},{9,5},{13... | collective-permute-start | bytes 491528 | tf_op jit(solution)/shard_map/ppermute | solution.py:24
  266.8 9.0 %collective-permute-start.14 = (bf16[320,3,1]{2,0,1:T(8,128)(2,1)S(1)}, bf16[320,3,1]{2,0,1:T(8,128)(2,1)S(1)}, u32[]{:S(2)}, u32[]{:S(2)}) collective-permute-start(bf16[320,3,1]{2,0,1:T(8,128)(2,1)S(1)} %get-tuple-element.20), channel_id=1, source_target_pairs={{0,1},{1,2},{2,3},{4,5},{5,6},{6,7},{8,9},{9,10},{10,11},{12,13},{... | collective-permute-start | bytes 5768 | tf_op jit(solution)/shard_map/ppermute | solution.py:22
  272.7 7.5 %collective-permute-start.15 = (bf16[320,3,1]{2,0,1:T(8,128)(2,1)S(1)}, bf16[320,3,1]{2,0,1:T(8,128)(2,1)S(1)}, u32[]{:S(2)}, u32[]{:S(2)}) collective-permute-start(bf16[320,3,1]{2,0,1:T(8,128)(2,1)S(1)} %get-tuple-element.19), channel_id=1, source_target_pairs={{1,0},{2,1},{3,2},{5,4},{6,5},{7,6},{9,8},{10,9},{11,10},{13,12},{... | collective-permute-start | bytes 5768 | tf_op jit(solution)/shard_map/ppermute | solution.py:24
  280.7 0.7 copy-start.9
Sparse Core Ops, SparseCore 0:
  8.9 32.2 all-gather.5
  43.4 79.4 all-gather.7
  124.5 21.1 all-gather.9
where the time goes:
time: 290 us; the launch traced here: 289 us
  blocking collectives  128 us (44%)
  starting transfers between devices  49 us (17%)
  waiting for transfers between devices  46.9 us (16%)
  local copies, waits for them, and re-layouts  25.6 us (9%)
  between operations  14.4 us (5%)
  other arithmetic  13.9 us (5%)
  matrix products  11.3 us (4%)
    psum x3, blocking collectives, norm_silu(): lax.psum((jnp.sum(grouped, axis=1), jnp.sum(grouped * grouped, axis=1)),...  118 us
    ppermute x8, starting transfers between devices, padded_2(): lax.ppermute(tail, axis, [(i, (i + 1) % count) for i in range(ends)])  35.6 us
    ppermute x8, waiting for transfers between devices, padded_2(): lax.ppermute(head, axis, [((i + 1) % count, i) for i in range(ends)])  30.7 us
    ppermute x8, starting transfers between devices, padded_2(): lax.ppermute(head, axis, [((i + 1) % count, i) for i in range(ends)])  13.3 us
    unnamed x41, local copies, waits for them, and re-layouts  12.7 us
    unnamed x23, other arithmetic  10.5 us
    all_gather x1, blocking collectives, shards(): lax.all_gather(skip_weight, 'cols', axis=0, tiled=True)  9.36 us
    ppermute x8, waiting for transfers between devices, padded_2(): lax.ppermute(tail, axis, [(i, (i + 1) % count) for i in range(ends)])  8.02 us
  transfers between devices with their start and end apart: 19, of which 12 were waited for; matrix products, arithmetic and copies ran while one was open for 15% of the time, Pallas kernels for 0%

commit v1 on v0

v1 whole, which is shorter than its diff:
```python
import functools
import math

import jax
import jax.numpy as jnp
from jax import lax
from jax.experimental import pallas as pl
from jax.experimental.pallas import tpu as pltpu
from jax.sharding import PartitionSpec as P

GROUPS = 32
EPS = 1e-05
TILE = 16
LANES = 128
MESH = pl.DeviceIdType.MESH
F32 = jnp.float32
BF16 = jnp.bfloat16
SIDES = tuple((i, j) for i in (-1, 0, 1) for j in (-1, 0, 1) if (i, j) != (0, 0))


def dot(a, b, precision=None):
    return lax.dot_general(
        a, b, (((1,), (0,)), ((), ())), preferred_element_type=F32, precision=precision
    )


def split_dot(row, weight):
    high = row.astype(BF16)
    rest = row - high.astype(F32)
    middle = rest.astype(BF16)
    low = (rest - middle.astype(F32)).astype(BF16)
    return dot(high, weight) + dot(middle, weight) + dot(low, weight)


def silu(z):
    return z / (1.0 + jnp.exp(-z))


def kernel(
    R, Q, ring,
    latent, deep, features, in_w, front, middle, skip, out_w, time_w, time_s, time_p,
    gain_one, gain_two, gain_three,
    noise,
    lat, jext, hext, oext, shifted, patch, fw, mw, sw, part, emb, sums_a, sums_b,
    lat_s, lat_r, halo_s, halo_r, fz_s, fy_s, fc_s, fm_r, fo_r, mid_s, mid_r, emb_s, emb_r,
    ca_s, ca_r, cb_s, cb_r, loc_s,
):
    r = lax.axis_index("rows")
    c = lax.axis_index("cols")
    C, px = deep.shape
    cin = latent.shape[0]
    image = float(px * R * Q)

    def remote(src, dst, ssem, rsem, rr, cc):
        return pltpu.make_async_remote_copy(
            src_ref=src, dst_ref=dst, send_sem=ssem, recv_sem=rsem,
            device_id={"rows": rr, "cols": cc}, device_id_type=MESH,
        )

    def each(count, body):
        if count <= 8:
            for i in range(1, count):
                body(i)
        else:
            lax.fori_loop(1, count, lambda i, u: (body(i), u)[1], 0)

    barrier = pltpu.get_barrier_semaphore()

    def greet(rr, cc):
        pl.semaphore_signal(barrier, inc=1, device_id={"rows": rr, "cols": cc}, device_id_type=MESH)

    each(R, lambda i: greet(lax.rem(r + i, R), c))
    each(Q, lambda i: greet(r, lax.rem(c + i, Q)))
    for i in (-1, 1):
        for j in (-1, 1):
            greet(lax.rem(r + i + R, R), lax.rem(c + j + Q, Q))
    pl.semaphore_wait(barrier, R - 1 + Q - 1 + 4)

    def inside(rr, cc):
        return (rr >= 0) & (rr < R) & (cc >= 0) & (cc < Q)

    def lat_copy(k, rr, cc):
        i, j = SIDES[k]
        return remote(latent, lat.at[k], lat_s.at[k], lat_r.at[k], rr, cc)

    for k, (i, j) in enumerate(SIDES):
        @pl.when(inside(r + i, c + j))
        def _():
            lat_copy(k, r + i, c + j).start()

        @pl.when(jnp.logical_not(inside(r - i, c - j)))
        def _():
            lat[k] = jnp.zeros(lat.shape[1:], lat.dtype)

    parity = lax.rem(c, 2)
    mate = c + 1 - 2 * parity
    over = lax.rem(c + 2, Q)
    half_c = lax.rem(r, 2)
    twin = r + 1 - 2 * half_c
    mk, sk = middle.shape[0], skip.shape[0]

    def mid_copies(owner, s, slot_from, target):
        rows_m = pl.ds(pl.multiple_of(owner * mk, TILE), mk)
        rows_s = pl.ds(pl.multiple_of(owner * sk, TILE), sk)
        src_m, src_s = (middle, skip) if slot_from else (mw.at[rows_m], sw.at[rows_s])
        return (
            remote(src_m, mw.at[rows_m], mid_s.at[0, s], mid_r.at[0, s], r, target),
            remote(src_s, sw.at[rows_s], mid_s.at[1, s], mid_r.at[1, s], r, target),
        )

    fk = fw.shape[0] // R if ring else 0
    cut = fk // 2 // TILE * TILE
    spans = ((0, cut), (cut, fk - cut))

    def f_rows(owner, par):
        return pl.ds(pl.multiple_of(owner * fk, TILE) + spans[par][0], spans[par][1])

    def by_parity(par_of, body):
        for par in (0, 1):
            @pl.when(par_of == par)
            def _():
                body(par)

    def f_own(par, target, ssem):
        src = front.at[pl.ds(spans[par][0], spans[par][1])]
        return remote(src, fw.at[f_rows(r, par)], ssem, fm_r.at[r], target, c)

    def f_pass(owner, par, target):
        return remote(fw.at[f_rows(owner, par)], fw.at[f_rows(owner, par)],
                      fy_s.at[owner], fm_r.at[owner], target, c)

    def f_mate(owner, par):
        return remote(fw.at[f_rows(owner, par)], fw.at[f_rows(owner, par)],
                      fc_s.at[owner], fo_r.at[owner], r, mate)

    locals_ = []
    if ring:
        locals_.append(pltpu.make_async_copy(
            front, fw.at[pl.ds(pl.multiple_of(r * fk, TILE), fk)], loc_s.at[0]))
    locals_.append(pltpu.make_async_copy(
        middle, mw.at[pl.ds(pl.multiple_of(c * mk, TILE), mk)], loc_s.at[1]))
    locals_.append(pltpu.make_async_copy(
        skip, sw.at[pl.ds(pl.multiple_of(c * sk, TILE), sk)], loc_s.at[2]))
    for copy in locals_:
        copy.start()

    if ring:
        def first(par):
            f_own(par, twin, fy_s.at[r]).start()
            for i in range(1, R // 2):
                t = lax.rem(r + 2 * i, R)
                f_own(par, t, fz_s.at[i]).start()
        by_parity(parity, first)
    for copy in mid_copies(c, 0, True, over) + mid_copies(c, 1, True, mate):
        copy.start()

    def pass_on(i):
        def go(par):
            owner = lax.rem(r + 2 * i, R)
            remote(fw.at[f_rows(owner, par)], fw.at[f_rows(owner, par)],
                   fz_s.at[i], fm_r.at[owner], r, c).wait_recv()
            f_pass(owner, par, twin).start()
            f_mate(owner, par).start()
        by_parity(parity, go)

    hidden = silu(split_dot(features[...], time_w[...]))
    tk = time_s.shape[0]
    for q in range(Q):
        @pl.when(c == q)
        def _():
            part[...] = hidden[:, q * tk : (q + 1) * tk]
    emb_own = split_dot(part[...], time_s[...])
    emb[c] = emb_own

    def emb_copy(i, src_c, tgt):
        return remote(emb.at[src_c], emb.at[src_c], emb_s.at[i], emb_r.at[i], r, tgt)

    for i in range(1, Q):
        emb_copy(i, c, lax.rem(c + i, Q)).start()

    for k, (i, j) in enumerate(SIDES):
        @pl.when(inside(r - i, c - j))
        def _():
            lat_copy(k, r - i, c - j).wait_recv()
    where = {side: k for k, side in enumerate(SIDES)}
    for a in range(3):
        tiles = []
        for b in range(3):
            side = (1 - a, 1 - b)
            block = latent[...] if side == (0, 0) else lat[where[side]]
            tiles.append(block.astype(F32))
        wide = jnp.concatenate(tiles, axis=1)
        for b in range(3):
            start = px + b - 1
            patch[cin * (3 * a + b) : cin * (3 * a + b + 1), :] = wide[:, start : start + px]
    skip_feat = dot(patch[...].T.astype(BF16), in_w[...]).astype(BF16)
    deep_t = deep[...].astype(F32).T.astype(BF16)
    own = pl.ds(TILE, px)
    jext[1, own, :] = jnp.concatenate([deep_t.astype(F32), skip_feat.astype(F32)], axis=1).astype(BF16)

    def halo_copy(stage, ext, k, rr, cc):
        i, j = SIDES[k]
        src = ((TILE, TILE), (TILE, px), (px, TILE))[j + 1]
        dst = ((TILE + px, TILE), (TILE, px), (0, TILE))[j + 1]
        return remote(ext.at[1, pl.ds(*src), :], ext.at[1 - i, pl.ds(*dst), :],
                      halo_s.at[stage, k], halo_r.at[stage, k], rr, cc)

    def halo_send(stage, ext):
        for k, (i, j) in enumerate(SIDES):
            @pl.when(inside(r + i, c + j))
            def _():
                halo_copy(stage, ext, k, r + i, c + j).start()

            @pl.when(jnp.logical_not(inside(r - i, c - j)))
            def _():
                dst = ((TILE + px, TILE), (TILE, px), (0, TILE))[j + 1]
                ext[1 - i, pl.ds(*dst), :] = jnp.zeros((dst[1], ext.shape[2]), ext.dtype)

    def halo_wait(stage, ext):
        for k, (i, j) in enumerate(SIDES):
            @pl.when(inside(r - i, c - j))
            def _():
                halo_copy(stage, ext, k, r - i, c - j).wait_recv()

    def indicator(channels, flip):
        shape = (LANES, channels) if flip else (channels, LANES)
        size = channels // GROUPS
        ch = lax.broadcasted_iota(jnp.int32, shape, 1 if flip else 0)
        g = lax.broadcasted_iota(jnp.int32, shape, 0 if flip else 1)
        return ((ch >= g * size) & (ch < g * size + size)).astype(F32)

    def sum_copy(buf, ssem, rsem, stage, slot, i, rr, cc):
        return remote(buf.at[stage, slot], buf.at[stage, slot],
                      ssem.at[stage, i], rsem.at[stage, i], rr, cc)

    def reduce_start(stage, values):
        top = jnp.sum(values, axis=0, keepdims=True)
        low = jnp.sum(values * values, axis=0, keepdims=True)
        both = jnp.concatenate([top, low, jnp.zeros((6, values.shape[1]), F32)], axis=0)
        sums_a[stage, c] = dot(both, indicator(values.shape[1], False), lax.Precision.HIGHEST)
        for i in range(1, Q):
            sum_copy(sums_a, ca_s, ca_r, stage, c, i, r, lax.rem(c + i, Q)).start()

    def reduce_end(stage, channels):
        for i in range(1, Q):
            s = lax.rem(c + Q - i, Q)
            sum_copy(sums_a, ca_s, ca_r, stage, s, i, r, s).wait_recv()
        sums_b[stage, r] = jnp.sum(sums_a[stage], axis=0)
        each(R, lambda i: sum_copy(sums_b, cb_s, cb_r, stage, r, i, lax.rem(r + i, R), c).start())

        def got(i):
            s = lax.rem(r + R - i, R)
            sum_copy(sums_b, cb_s, cb_r, stage, s, i, s, c).wait_recv()

        each(R, got)
        total = jnp.sum(sums_b[stage], axis=0) / (channels // GROUPS * image)
        center = total[0:1]
        inverse = lax.rsqrt(total[1:2] - center * center + EPS)
        both = jnp.concatenate([center, inverse, jnp.zeros((6, LANES), F32)], axis=0)
        wide = dot(both, indicator(channels, True), lax.Precision.HIGHEST)
        return wide[0:1], wide[1:2]

    def conv(stage, ext, stats, gain, weight):
        center, inverse = stats
        channels = ext.shape[2]
        scale = inverse * gain[...]
        place = lax.broadcasted_iota(jnp.int32, (px + 2 * TILE, 1), 0)
        inner = (place >= TILE) & (place < TILE + px)
        total = None
        for a in (1, 0, 2):
            z = (ext[a].astype(F32) - center) * scale
            here = r + a - 1
            keep = (here >= 0) & (here < R) & (
                inner | ((place < TILE) & (c > 0)) | ((place >= TILE + px) & (c < Q - 1)))
            shifted[:, 0:channels] = jnp.where(keep, silu(z), 0.0)
            for b in range(3):
                act = shifted[TILE + b - 1 : TILE + b - 1 + px, 0:channels].astype(BF16)
                k = (3 * a + b) * channels
                term = dot(act, weight[k : k + channels, :])
                total = term if total is None else total + term
        return total

    joined = jext[1, own, :]
    reduce_start(0, joined.astype(F32))
    halo_send(0, jext)

    if ring:
        order = list(range(1, R // 2))
        for i in order[:1]:
            pass_on(i)
    stats = reduce_end(0, 2 * C)
    if ring:
        for i in order[1:]:
            pass_on(i)

        def from_twin(i):
            def go(par):
                owner = lax.rem(twin + 2 * i, R)
                f_pass(owner, par, twin).wait_recv()
                f_mate(owner, par).start()
            by_parity(parity, go)

        for i in range(R // 2):
            from_twin(i)

    for copy in mid_copies(over, 0, False, over):
        copy.wait_recv()
    for copy in mid_copies(over, 2, False, mate):
        copy.start()

    for i in range(1, Q):
        s = lax.rem(c + Q - i, Q)
        emb_copy(i, s, s).wait_recv()
    embedded = jnp.sum(emb[...], axis=0)
    time_shift = split_dot(silu(embedded), time_p[...])

    for copy in locals_:
        copy.wait()
    halo_wait(0, jext)
    if ring:
        def from_mate(i):
            owner = lax.rem(r + i, R)
            def go(par):
                f_mate(owner, 1 - par).wait_recv()
            by_parity(parity, go)
        for i in range(1, R):
            from_mate(i)
    hidden_one = conv(0, jext, stats, gain_one, fw if ring else front) + time_shift

    hext[1, own, :] = hidden_one.astype(BF16)
    reduce_start(1, hidden_one)
    halo_send(1, hext)
    for copy in mid_copies(mate, 1, False, mate):
        copy.wait_recv()
    far = lax.rem(mate + 2, Q)
    for copy in mid_copies(far, 2, False, mate):
        copy.wait_recv()
    shortcut = dot(joined, sw[...])
    stats = reduce_end(1, C)
    halo_wait(1, hext)
    block_out = conv(1, hext, stats, gain_two, mw) + shortcut

    oext[1, own, :] = block_out.astype(BF16)
    reduce_start(2, block_out)
    halo_send(2, oext)
    stats = reduce_end(2, C)
    halo_wait(2, oext)
    result = conv(2, oext, stats, gain_three, out_w)
    noise[...] = result.T[0 : noise.shape[0], :]

    for k, (i, j) in enumerate(SIDES):
        @pl.when(inside(r + i, c + j))
        def _():
            lat_copy(k, r + i, c + j).wait_send()
            for stage, ext in enumerate((jext, hext, oext)):
                halo_copy(stage, ext, k, r + i, c + j).wait_send()
    for i in range(1, Q):
        emb_copy(i, c, lax.rem(c + i, Q)).wait_send()
        for stage in range(3):
            sum_copy(sums_a, ca_s, ca_r, stage, c, i, r, lax.rem(c + i, Q)).wait_send()

    def sent(i):
        for stage in range(3):
            sum_copy(sums_b, cb_s, cb_r, stage, r, i, lax.rem(r + i, R), c).wait_send()

    each(R, sent)
    for copy in (mid_copies(c, 0, True, over) + mid_copies(c, 1, True, mate)
                 + mid_copies(over, 2, False, mate)):
        copy.wait_send()
    if ring:
        def last(par):
            f_own(par, twin, fy_s.at[r]).wait_send()
            for i in range(1, R // 2):
                f_own(par, lax.rem(r + 2 * i, R), fz_s.at[i]).wait_send()
                f_pass(lax.rem(r + 2 * i, R), par, twin).wait_send()
            for i in range(1, R):
                f_mate(lax.rem(r + i, R), par).wait_send()
        by_parity(parity, last)


def shards(
    R, Q,
    latent, deep, timestep, in_weight, front_weight, middle_weight, skip_weight, out_weight,
    time_weight, time_second, time_proj, input_gain, middle_gain, output_gain,
):
    C = deep.shape[0]
    cin = latent.shape[0]
    px = deep.shape[1] * deep.shape[2]
    assert deep.shape[1] == 1 and Q == 4 and R % 2 == 0 and R > 2
    ring = R <= 8 and front_weight.shape[0] % TILE == 0
    half = time_weight.shape[0] // 2
    ratios = jnp.exp(-math.log(10000.0) * jnp.arange(half, dtype=F32) / half)
    angles = timestep[0].astype(F32) * ratios
    features = jnp.concatenate([jnp.cos(angles), jnp.sin(angles)])[None, :]
    front = front_weight if ring else lax.all_gather(front_weight, "rows", axis=0, tiled=True)
    couts = out_weight.shape[1]
    out_w = jnp.pad(out_weight, ((0, 0), (0, LANES - couts)))
    vmem = pl.BlockSpec(memory_space=pltpu.VMEM)
    dma = pltpu.SemaphoreType.DMA
    wide = time_second.shape[1]
    tall = px + 2 * TILE
    args = (
        latent.reshape(cin, px), deep.reshape(C, px), features, in_weight, front,
        middle_weight, skip_weight, out_w, time_weight, time_second, time_proj,
        input_gain[None, :], middle_gain[None, :], output_gain[None, :],
    )
    out = pl.pallas_call(
        functools.partial(kernel, R, Q, ring),
        out_shape=jax.ShapeDtypeStruct((couts, px), F32),
        in_specs=[vmem] * len(args),
        out_specs=vmem,
        scratch_shapes=[
            pltpu.VMEM((8, cin, px), BF16),
            pltpu.VMEM((3, tall, 2 * C), BF16),
            pltpu.VMEM((3, tall, C), BF16),
            pltpu.VMEM((3, tall, C), BF16),
            pltpu.VMEM((tall, 2 * C), F32),
            pltpu.VMEM((9 * cin, px), F32),
            pltpu.VMEM((18 * C if ring else TILE, C), BF16),
            pltpu.VMEM((9 * C, C), BF16),
            pltpu.VMEM((2 * C, C), BF16),
            pltpu.VMEM((1, time_second.shape[0]), F32),
            pltpu.VMEM((Q, 1, wide), F32),
            pltpu.VMEM((3, Q, 8, LANES), F32),
            pltpu.VMEM((3, R, 8, LANES), F32),
            dma((8,)), dma((8,)), dma((3, 8)), dma((3, 8)),
            dma((R,)), dma((R,)), dma((R,)), dma((R,)), dma((R,)),
            dma((2, 3)), dma((2, 3)), dma((Q,)), dma((Q,)),
            dma((3, Q)), dma((3, Q)), dma((3, R)), dma((3, R)), dma((3,)),
        ],
        compiler_params=pltpu.CompilerParams(
            collective_id=0, has_side_effects=True, vmem_limit_bytes=56 * 1024 * 1024
        ),
    )(*args)
    return out.reshape(couts, 1, px)


def solution(mesh):
    R, Q = mesh.shape["rows"], mesh.shape["cols"]
    return jax.shard_map(
        functools.partial(shards, R, Q),
        mesh=mesh,
        in_specs=(
            P(None, "rows", "cols"), P(None, "rows", "cols"), P(), P(),
            P("rows", None), P("cols", None), P("cols", None), P(),
            P(), P("cols", None), P(), P(), P(), P(),
        ),
        out_specs=P(None, "rows", "cols"),
        check_vma=False,
    )
```

time: 290 us -> 105 us (0.36)
  the two profiles are of different devices: /device:TPU:1 before, /device:TPU:11 now
where the time goes in v1:
time: 105 us
  Pallas kernels  93.5 us (89%)
  local copies, waits for them, and re-layouts  10.6 us (10%)
    pallas_call x1, Pallas kernels, shards(): pl.pallas_call(functools.partial(kernel, R, Q, ring), out_shape=jax.Shape...  93.5 us
    unnamed x16, local copies, waits for them, and re-layouts  6.05 us

profile of v1, /device:TPU:11, one launch (start us, length us, event | category | flops | bytes accessed | tf_op | source)
XLA Modules:
  0.0 104.9 jit_solution(7881790211256894341)
XLA Ops:
  0.7 0.0 copy-start.4
  0.7 0.7 copy-done.4
  1.3 0.0 copy-start.5
  1.3 0.5 broadcast_in_dim.14.gain_two
  1.9 0.2 copy-done.5
  2.0 0.6 broadcast_in_dim.15.gain_three
  2.7 0.0 copy-start.3
  2.7 0.1 pad_maximum_fusion
  2.7 0.5 broadcast_in_dim.12.features
  3.3 0.1 copy-done.3
  3.4 0.6 broadcast_in_dim.13.gain_one
  3.9 0.0 copy-start.1
  3.9 2.1 %copy.16.front = bf16[720,320]{1,0:T(8,128)(2,1)} copy(bf16[720,320]{0,1:T(8,128)(2,1)} %param.18) | data formatting | bytes 921600 | tf_op args[4]
  6.1 0.0 copy-done.1
  6.1 0.0 copy-start.2
  6.1 1.0 copy.17.middle
  7.1 0.0 copy-done.2
  7.1 0.4 copy.15
  7.5 0.0 copy-start
  7.5 1.1 %pad.4.out_w = bf16[2880,128]{1,0:T(8,128)(2,1)} pad(bf16[2880,4]{1,0:T(8,128)(2,1)S(1)} %copy.15, bf16[]{:T(256)} %constant.7.clone.1), padding=0_0x0_124 | pad | bytes 760322 | tf_op jit(solution)/shard_map/jit(_pad)/pad | solution.py:397
  8.6 0.3 copy-done
  8.9 1.3 %copy.18.time_p = bf16[1280,320]{1,0:T(8,128)(2,1)} copy(bf16[1280,320]{0,1:T(8,128)(2,1)S(1)} %copy-done) | data formatting | bytes 1638400 | tf_op args[10]
  10.2 93.5 %shard_map.136 = f32[4,256]{1,0:T(4,128)} custom-call(bf16[4,256]{1,0:T(4,128)(2,1)} %bitcast.6, bf16[320,256]{1,0:T(8,128)(2,1)} %bitcast.4, f32[1,320]{1,0:T(1,128)} %broadcast_in_dim.12.features, bf16[36,320]{1,0:T(8,128)(2,1)} %in_w.1, bf16[720,320]{1,0:T(8,128)(2,1)} %copy.16.front, bf16[720,320]{1,0:T(8,128)(2,1)} %copy.17.middle, ...), custom_call_target="tpu_custom_call" | custom-call | tf_op jit(solution)/shard_map/pallas_call | solution.py:407
  103.7 1.3 %copy.19 = f32[4,1,256]{2,1,0:T(1,128)} copy(f32[4,1,256]{2,0,1:T(4,128)} %bitcast.5) | data formatting | bytes 8192 | tf_op jit(solution)/shard_map/reshape | solution.py:435
  (1 shorter events, 0.0 us)
Async XLA Ops:
  0.7 0.7 copy-start.4
  1.3 0.7 copy-start.5
  2.7 0.7 copy-start.3
  3.9 2.1 %copy-start.1 = (bf16[720,320]{0,1:T(8,128)(2,1)S(1)}, bf16[720,320]{0,1:T(8,128)(2,1)}, u32[]{:S(2)}) copy-start(bf16[720,320]{0,1:T(8,128)(2,1)} %param.19) | copy-start | bytes 1382404
  6.1 1.0 copy-start.2
  7.5 1.3 %copy-start = (bf16[1280,320]{0,1:T(8,128)(2,1)S(1)}, bf16[1280,320]{0,1:T(8,128)(2,1)}, u32[]{:S(2)}) copy-start(bf16[1280,320]{0,1:T(8,128)(2,1)} %param.24) | copy-start | bytes 2457604

commit v2 on v1

--- a/solution.py
+++ b/solution.py
@@ -29,7 +29,8 @@
     rest = row - high.astype(F32)
     middle = rest.astype(BF16)
     low = (rest - middle.astype(F32)).astype(BF16)
-    return dot(high, weight) + dot(middle, weight) + dot(low, weight)
+    pieces = jnp.concatenate([high.astype(F32), middle.astype(F32), low.astype(F32)], axis=0)
+    return jnp.sum(dot(pieces.astype(BF16), weight), axis=0, keepdims=True)
 
 
 def silu(z):
@@ -38,8 +39,7 @@
 
 def kernel(
     R, Q, ring,
-    latent, deep, features, in_w, front, middle, skip, out_w, time_w, time_s, time_p,
-    gain_one, gain_two, gain_three,
+    latent, deep, rows_in, in_w, front, middle, skip, out_w, time_w, time_s, time_p,
     noise,
     lat, jext, hext, oext, shifted, patch, fw, mw, sw, part, emb, sums_a, sums_b,
     lat_s, lat_r, halo_s, halo_r, fz_s, fy_s, fc_s, fm_r, fo_r, mid_s, mid_r, emb_s, emb_r,
@@ -50,6 +50,10 @@
     C, px = deep.shape
     cin = latent.shape[0]
     image = float(px * R * Q)
+    FQ = time_w.shape[0]
+    gain_one = rows_in[:, FQ : FQ + 2 * C]
+    gain_two = rows_in[:, FQ + 2 * C : FQ + 3 * C]
+    gain_three = rows_in[:, FQ + 3 * C : FQ + 4 * C]
 
     def remote(src, dst, ssem, rsem, rr, cc):
         return pltpu.make_async_remote_copy(
@@ -133,6 +137,13 @@
         return remote(fw.at[f_rows(owner, par)], fw.at[f_rows(owner, par)],
                       fc_s.at[owner], fo_r.at[owner], r, mate)
 
+    def by_distance(distances, body):
+        for d in distances:
+            for t in (r + 2 * d, r - 2 * d):
+                @pl.when((t >= 0) & (t < R))
+                def _():
+                    body(t)
+
     locals_ = []
     if ring:
         locals_.append(pltpu.make_async_copy(
@@ -147,36 +158,21 @@
     if ring:
         def first(par):
             f_own(par, twin, fy_s.at[r]).start()
-            for i in range(1, R // 2):
-                t = lax.rem(r + 2 * i, R)
-                f_own(par, t, fz_s.at[i]).start()
+            def one(t):
+                f_own(par, t, fz_s.at[t]).start()
+            by_distance(range(1, R // 2), one)
         by_parity(parity, first)
     for copy in mid_copies(c, 0, True, over) + mid_copies(c, 1, True, mate):
         copy.start()
 
-    def pass_on(i):
+    def pass_on(distances):
         def go(par):
-            owner = lax.rem(r + 2 * i, R)
-            remote(fw.at[f_rows(owner, par)], fw.at[f_rows(owner, par)],
-                   fz_s.at[i], fm_r.at[owner], r, c).wait_recv()
-            f_pass(owner, par, twin).start()
-            f_mate(owner, par).start()
+            def one(owner):
+                f_pass(owner, par, twin).wait_recv()
+                f_pass(owner, par, twin).start()
+                f_mate(owner, par).start()
+            by_distance(distances, one)
         by_parity(parity, go)
-
-    hidden = silu(split_dot(features[...], time_w[...]))
-    tk = time_s.shape[0]
-    for q in range(Q):
-        @pl.when(c == q)
-        def _():
-            part[...] = hidden[:, q * tk : (q + 1) * tk]
-    emb_own = split_dot(part[...], time_s[...])
-    emb[c] = emb_own
-
-    def emb_copy(i, src_c, tgt):
-        return remote(emb.at[src_c], emb.at[src_c], emb_s.at[i], emb_r.at[i], r, tgt)
-
-    for i in range(1, Q):
-        emb_copy(i, c, lax.rem(c + i, Q)).start()
 
     for k, (i, j) in enumerate(SIDES):
         @pl.when(inside(r - i, c - j))
@@ -260,10 +256,12 @@
         wide = dot(both, indicator(channels, True), lax.Precision.HIGHEST)
         return wide[0:1], wide[1:2]
 
-    def conv(stage, ext, stats, gain, weight):
+    def conv(ext, stats, gain, weight, exact=None, shift=None):
         center, inverse = stats
+        if shift is not None:
+            center = center - shift
         channels = ext.shape[2]
-        scale = inverse * gain[...]
+        scale = inverse * gain
         place = lax.broadcasted_iota(jnp.int32, (px + 2 * TILE, 1), 0)
         inner = (place >= TILE) & (place < TILE + px)
         total = None
@@ -273,6 +271,8 @@
             keep = (here >= 0) & (here < R) & (
                 inner | ((place < TILE) & (c > 0)) | ((place >= TILE + px) & (c < Q - 1)))
             shifted[:, 0:channels] = jnp.where(keep, silu(z), 0.0)
+            if a == 1 and exact is not None:
+                shifted[own, 0:channels] = silu((exact - center) * scale)
             for b in range(3):
                 act = shifted[TILE + b - 1 : TILE + b - 1 + px, 0:channels].astype(BF16)
                 k = (3 * a + b) * channels
@@ -284,24 +284,35 @@
     reduce_start(0, joined.astype(F32))
     halo_send(0, jext)
 
-    if ring:
-        order = list(range(1, R // 2))
-        for i in order[:1]:
-            pass_on(i)
+    hidden = silu(split_dot(rows_in[:, 0:FQ], time_w[...]))
+    tk = time_s.shape[0]
+    for q in range(Q):
+        @pl.when(c == q)
+        def _():
+            part[...] = hidden[:, q * tk : (q + 1) * tk]
+    emb_own = split_dot(part[...], time_s[...])
+    emb[c] = emb_own
+
+    def emb_copy(i, src_c, tgt):
+        return remote(emb.at[src_c], emb.at[src_c], emb_s.at[i], emb_r.at[i], r, tgt)
+
+    for i in range(1, Q):
+        emb_copy(i, c, lax.rem(c + i, Q)).start()
+
+    if ring:
+        pass_on((1,))
     stats = reduce_end(0, 2 * C)
     if ring:
-        for i in order[1:]:
-            pass_on(i)
-
-        def from_twin(i):
-            def go(par):
-                owner = lax.rem(twin + 2 * i, R)
+        pass_on(range(2, R // 2))
+
+        def from_twin(par):
+            def one(t):
+                owner = t + twin - r
                 f_pass(owner, par, twin).wait_recv()
                 f_mate(owner, par).start()
-            by_parity(parity, go)
-
-        for i in range(R // 2):
-            from_twin(i)
+            one(r)
+            by_distance(range(1, R // 2), one)
+        by_parity(parity, from_twin)
 
     for copy in mid_copies(over, 0, False, over):
         copy.wait_recv()
@@ -325,10 +336,10 @@
             by_parity(parity, go)
         for i in range(1, R):
             from_mate(i)
-    hidden_one = conv(0, jext, stats, gain_one, fw if ring else front) + time_shift
-
-    hext[1, own, :] = hidden_one.astype(BF16)
-    reduce_start(1, hidden_one)
+    front_out = conv(jext, stats, gain_one, fw if ring else front)
+
+    hext[1, own, :] = front_out.astype(BF16)
+    reduce_start(1, front_out + time_shift)
     halo_send(1, hext)
     for copy in mid_copies(mate, 1, False, mate):
         copy.wait_recv()
@@ -338,14 +349,14 @@
     shortcut = dot(joined, sw[...])
     stats = reduce_end(1, C)
     halo_wait(1, hext)
-    block_out = conv(1, hext, stats, gain_two, mw) + shortcut
+    block_out = conv(hext, stats, gain_two, mw, front_out, time_shift) + shortcut
 
     oext[1, own, :] = block_out.astype(BF16)
     reduce_start(2, block_out)
     halo_send(2, oext)
     stats = reduce_end(2, C)
     halo_wait(2, oext)
-    result = conv(2, oext, stats, gain_three, out_w)
+    result = conv(oext, stats, gain_three, out_w, block_out)
     noise[...] = result.T[0 : noise.shape[0], :]
 
     for k, (i, j) in enumerate(SIDES):
@@ -370,9 +381,10 @@
     if ring:
         def last(par):
             f_own(par, twin, fy_s.at[r]).wait_send()
-            for i in range(1, R // 2):
-                f_own(par, lax.rem(r + 2 * i, R), fz_s.at[i]).wait_send()
-                f_pass(lax.rem(r + 2 * i, R), par, twin).wait_send()
+            def one(t):
+                f_own(par, t, fz_s.at[t]).wait_send()
+                f_pass(t, par, twin).wait_send()
+            by_distance(range(1, R // 2), one)
             for i in range(1, R):
                 f_mate(lax.rem(r + i, R), par).wait_send()
         by_parity(parity, last)
@@ -391,7 +403,8 @@
     half = time_weight.shape[0] // 2
     ratios = jnp.exp(-math.log(10000.0) * jnp.arange(half, dtype=F32) / half)
     angles = timestep[0].astype(F32) * ratios
-    features = jnp.concatenate([jnp.cos(angles), jnp.sin(angles)])[None, :]
+    rows_in = jnp.concatenate(
+        [jnp.cos(angles), jnp.sin(angles), input_gain, middle_gain, output_gain])[None, :]
     front = front_weight if ring else lax.all_gather(front_weight, "rows", axis=0, tiled=True)
     couts = out_weight.shape[1]
     out_w = jnp.pad(out_weight, ((0, 0), (0, LANES - couts)))
@@ -400,9 +413,8 @@
     wide = time_second.shape[1]
     tall = px + 2 * TILE
     args = (
-        latent.reshape(cin, px), deep.reshape(C, px), features, in_weight, front,
+        latent.reshape(cin, px), deep.reshape(C, px), rows_in, in_weight, front,
         middle_weight, skip_weight, out_w, time_weight, time_second, time_proj,
-        input_gain[None, :], middle_gain[None, :], output_gain[None, :],
     )
     out = pl.pallas_call(
         functools.partial(kernel, R, Q, ring),

time: 105 us -> 92.9 us (0.88)
  the two profiles are of different devices: /device:TPU:11 before, /device:TPU:1 now
where the time goes in v2:
time: 92.9 us; the launch traced here: 91.1 us
  Pallas kernels  81.5 us (88%)
  local copies, waits for them, and re-layouts  8.84 us (10%)
    pallas_call x1, Pallas kernels, shards(): pl.pallas_call(functools.partial(kernel, R, Q, ring), out_shape=jax.Shape...  81.5 us
    unnamed x16, local copies, waits for them, and re-layouts  5.83 us

profile of v2, /device:TPU:1, one launch (start us, length us, event | category | flops | bytes accessed | tf_op | source)
XLA Modules:
  0.0 91.1 jit_solution(17739386106113357649)
XLA Ops:
  0.7 0.0 copy-start.3
  0.7 0.0 copy-start.5
  0.7 0.0 copy-start.4
  0.7 0.6 copy-done.3
  1.3 0.0 copy-done.5
  1.4 0.1 copy-done.4
  1.4 0.1 concatenate.3
  1.5 0.6 broadcast_in_dim.3.rows_in
  2.1 0.0 copy-start.1
  2.1 2.1 %copy.16.front = bf16[720,320]{1,0:T(8,128)(2,1)} copy(bf16[720,320]{0,1:T(8,128)(2,1)} %param.18) | data formatting | bytes 921600 | tf_op args[4]
  4.2 0.0 copy-done.1
  4.2 0.0 copy-start.2
  4.2 1.0 %copy.17.middle = bf16[720,320]{1,0:T(8,128)(2,1)} copy(bf16[720,320]{0,1:T(8,128)(2,1)S(1)} %copy-done.1) | data formatting | bytes 921600 | tf_op args[5]
  5.3 0.0 copy-done.2
  5.3 0.4 copy.15
  5.7 0.0 copy-start
  5.7 1.1 %pad.4.out_w = bf16[2880,128]{1,0:T(8,128)(2,1)} pad(bf16[2880,4]{1,0:T(8,128)(2,1)S(1)} %copy.15, bf16[]{:T(256)} %constant.7.clone.1), padding=0_0x0_124 | pad | bytes 760322 | tf_op jit(solution)/shard_map/jit(_pad)/pad | solution.py:410
  6.8 0.3 copy-done
  7.0 1.3 %copy.18.time_p = bf16[1280,320]{1,0:T(8,128)(2,1)} copy(bf16[1280,320]{0,1:T(8,128)(2,1)S(1)} %copy-done) | data formatting | bytes 1638400 | tf_op args[10]
  8.3 81.5 %shard_map.136 = f32[4,256]{1,0:T(4,128)} custom-call(bf16[4,256]{1,0:T(4,128)(2,1)} %bitcast.6, bf16[320,256]{1,0:T(8,128)(2,1)} %bitcast.4, f32[1,1600]{1,0:T(1,128)} %broadcast_in_dim.3.rows_in, bf16[36,320]{1,0:T(8,128)(2,1)} %in_w.1, bf16[720,320]{1,0:T(8,128)(2,1)} %copy.16.front, bf16[720,320]{1,0:T(8,128)(2,1)} %copy.17.middle, ...), custom_call_target="tpu_custom_call" | custom-call | tf_op jit(solution)/shard_map/pallas_call | solution.py:419
  89.8 1.3 %copy.19 = f32[4,1,256]{2,1,0:T(1,128)} copy(f32[4,1,256]{2,0,1:T(4,128)} %bitcast.5) | data formatting | bytes 8192 | tf_op jit(solution)/shard_map/reshape | solution.py:447
  (1 shorter events, 0.0 us)
Async XLA Ops:
  0.7 0.7 copy-start.3
  0.7 0.7 copy-start.5
  0.7 0.7 copy-start.4
  2.1 2.1 %copy-start.1 = (bf16[720,320]{0,1:T(8,128)(2,1)S(1)}, bf16[720,320]{0,1:T(8,128)(2,1)}, u32[]{:S(2)}) copy-start(bf16[720,320]{0,1:T(8,128)(2,1)} %param.19) | copy-start | bytes 1382404
  4.2 1.0 %copy-start.2 = (bf16[2880,4]{0,1:T(4,128)(2,1)S(1)}, bf16[2880,4]{0,1:T(4,128)(2,1)}, u32[]{:S(2)}) copy-start(bf16[2880,4]{0,1:T(4,128)(2,1)} %param.21) | copy-start | bytes 69124
  5.7 1.3 %copy-start = (bf16[1280,320]{0,1:T(8,128)(2,1)S(1)}, bf16[1280,320]{0,1:T(8,128)(2,1)}, u32[]{:S(2)}) copy-start(bf16[1280,320]{0,1:T(8,128)(2,1)} %param.24) | copy-start | bytes 2457604
